TPU v7x, 256 devices: a whole 4x4x8 slice. The times are simulated.
256 devices in a mesh: row: 8 (over y, core), col: 8 (over z), depth: 4 (over x).
Axes of the slice: x: 4, y: 4, z: 8, core: 2. Of those that a mesh axis runs over, the one named last changes fastest.
Arguments:
- matrix: float32 [4, 8, 512, 16384], P(None, 'row', None, ('col', 'depth')), as said below
Outputs:
- factored: float32 [4, 8, 512, 16384], P(None, 'row', None, ('col', 'depth'))
Inputs may be any that keep to these rules, and one draw needn't show every extreme that they name: matrix is symmetric positive definite.
All inputs are finite; a program needn't handle non-finite values.
Results may differ from a plain program's by a relative error of at most 0.0001.
Values sent between devices are 32-bit elements; how exact they have to be, the bound alone decides.
A program may use at most 128 MiB of HBM per device.

v0:
```python
import jax
import jax.numpy as jnp
from jax import lax
from jax.sharding import PartitionSpec as P

PANELS = 2


def broadcast(x, axis, root):
    return lax.dynamic_index_in_dim(lax.all_gather(x, axis), root, 0, keepdims=False)


def spread(x, axis, root):
    mine = lax.axis_index(axis) == root
    return lax.psum(jnp.where(mine, x, jnp.zeros_like(x)), axis)


def factor_blocks(lower_factor, blocks, block_ids, panel_index):
    count_rows, block_size, _ = blocks.shape
    solved = lax.linalg.triangular_solve(
        lower_factor,
        blocks.reshape(count_rows * block_size, block_size),
        left_side=False,
        lower=True,
        transpose_a=True,
    )
    solved = solved.reshape(count_rows, block_size, block_size)
    marks = block_ids[:, None, None]
    return jnp.where(
        marks > panel_index,
        solved,
        jnp.where(marks == panel_index, lower_factor[None], jnp.float32(0.0)),
    )


def body(matrix):
    blocks_here = matrix[:, 0, :, :]
    count_rows = blocks_here.shape[0]
    block_size = blocks_here.shape[1]
    row_count = lax.axis_size("row")
    my_row = lax.axis_index("row")
    my_column = lax.axis_index(("col", "depth"))
    block_ids = jnp.arange(count_rows, dtype=jnp.int32) * row_count + my_row
    cross_slot = my_column // row_count
    cross_owner = my_column % row_count
    identity = jnp.eye(block_size, dtype=jnp.float32)
    for panel_index in range(PANELS):
        diag_slot = panel_index // row_count
        diag_owner = panel_index % row_count
        diag_raw = broadcast(blocks_here[diag_slot], "row", diag_owner)
        diag_raw = jnp.where(my_column == panel_index, diag_raw, identity)
        lower_factor = jnp.linalg.cholesky(diag_raw)
        own_panel = factor_blocks(lower_factor, blocks_here, block_ids, panel_index)
        panel_blocks = spread(own_panel, ("col", "depth"), panel_index)
        picked = lax.dynamic_index_in_dim(panel_blocks, cross_slot, 0, keepdims=False)
        cross_block = broadcast(picked, "row", cross_owner)
        update = blocks_here - jnp.einsum(
            "axy,zy->axz", panel_blocks, cross_block, precision=lax.Precision.HIGHEST
        )
        trailing = jnp.where(block_ids[:, None, None] > panel_index, update, jnp.float32(0.0))
        blocks_here = jnp.where(
            my_column > panel_index,
            trailing,
            jnp.where(my_column == panel_index, panel_blocks, blocks_here),
        )
    return blocks_here[:, None, :, :]


def solution(mesh):
    placed = (P(None, "row", None, ("col", "depth")),)
    return jax.shard_map(
        body,
        mesh=mesh,
        in_specs=placed,
        out_specs=P(None, "row", None, ("col", "depth")),
        check_vma=False,
    )
```

profile of v0, /device:TPU:19, one launch (start us, length us, event | category | flops | bytes accessed | tf_op | source)
XLA Modules:
  0.0 921.0 jit_solution(8789543255819709000)
XLA Ops:
  8.9 54.6 %all-gather.12.cloned.1.call-done = f32[8,1,512,512]{3,2,1,0:T(8,128)} async-done(((f32[1,1,512,512]{3,2,1,0:T(8,128)}), f32[8,1,512,512]{3,2,1,0:T(8,128)}) %all-gather.12.cloned.1.call-update) | async-done | bytes 8388624 | tf_op jit(solution)/shard_map/all_gather | solution.py:10
  65.9 11.7 %cholesky.286 = f32[128,128]{1,0:T(8,128)S(1)} custom-call(f32[128,128]{1,0:T(8,128)S(1)} %cholesky.426), custom_call_target="Cholesky" | custom-call | tf_op jit(solution)/shard_map/jit(cholesky)/cholesky | solution.py:52
  77.6 9.8 %custom-call.27 = f32[1,128,128]{1,2,0:T(8,128)S(1)} custom-call(f32[1,128,128]{2,1,0:T(8,128)S(1)} %get-tuple-element.66), custom_call_target="InvertDiagBlocksLowerTriangular" | custom-call | tf_op jit(solution)/shard_map/jit(cholesky)/cholesky | solution.py:52
  88.2 11.7 %cholesky.305 = f32[128,128]{1,0:T(8,128)S(1)} custom-call(f32[128,128]{1,0:T(8,128)S(1)} %cholesky.430), custom_call_target="Cholesky" | custom-call | tf_op jit(solution)/shard_map/jit(cholesky)/cholesky | solution.py:52
  100.0 10.0 %custom-call.28 = f32[1,128,128]{1,2,0:T(8,128)S(1)} custom-call(f32[1,128,128]{2,1,0:T(8,128)S(1)} %get-tuple-element.63), custom_call_target="InvertDiagBlocksLowerTriangular" | custom-call | tf_op jit(solution)/shard_map/jit(cholesky)/cholesky | solution.py:52
  110.7 11.7 %cholesky.326 = f32[128,128]{1,0:T(8,128)S(1)} custom-call(f32[128,128]{1,0:T(8,128)S(1)} %cholesky.435), custom_call_target="Cholesky" | custom-call | tf_op jit(solution)/shard_map/jit(cholesky)/cholesky | solution.py:52
  123.1 9.8 %custom-call.29 = f32[1,128,128]{1,2,0:T(8,128)S(1)} custom-call(f32[1,128,128]{2,1,0:T(8,128)S(1)} %get-tuple-element.60), custom_call_target="InvertDiagBlocksLowerTriangular" | custom-call | tf_op jit(solution)/shard_map/jit(cholesky)/cholesky | solution.py:52
  133.5 22.2 %cholesky.343 = f32[128,128]{1,0:T(8,128)S(1)} custom-call(f32[128,128]{1,0:T(8,128)S(1)} %convolution_subtract_fusion.9), custom_call_target="Cholesky" | custom-call | tf_op jit(solution)/shard_map/jit(cholesky)/cholesky | solution.py:52
  159.8 8.0 while.4
  167.8 39.3 %custom-call.30 = f32[4,128,128]{1,2,0:T(8,128)S(1)} custom-call(f32[4,128,128]{2,1,0:T(8,128)S(1)} %get-tuple-element.21), custom_call_target="InvertDiagBlocksLowerTriangular" | custom-call | tf_op jit(solution)/shard_map/triangular_solve/custom-call.3 | solution.py:20
  218.3 5.6 fusion.17
  227.5 5.3 copy.33
  232.9 4.9 select_select_fusion.1
  237.9 161.1 %all-reduce.4.cloned.1.call-done = f32[4,512,512]{2,1,0:T(8,128)} async-done(((f32[4,512,512]{2,1,0:T(8,128)}), f32[4,512,512]{2,1,0:T(8,128)}) %all-reduce.4.cloned.1.call-update) | async-done | bytes 4194320 | tf_op jit(solution)/shard_map/psum | solution.py:15
  401.4 53.0 %all-gather.6.cloned.1.call-done = f32[8,512,512]{2,1,0:T(8,128)} async-done(((f32[1,512,512]{2,1,0:T(8,128)}), f32[8,512,512]{2,1,0:T(8,128)}) %all-gather.6.cloned.1.call-update) | async-done | bytes 8388624 | tf_op jit(solution)/shard_map/all_gather | solution.py:10
  454.4 10.5 %fusion.1 = f32[4,512,512]{2,1,0:T(8,128)S(1)} fusion(f32[4,1,512,512]{3,2,1,0:T(8,128)} %param.4, f32[4,512,512]{2,1,0:T(8,128)} %all-reduce.4.cloned.1.call-done, pred[4]{0:T(512)(128)(4,1)S(1)} %get-tuple-element.72, pred[]{:T(512)S(6)} %eq.33, pred[]{:T(512)S(6)} %gt.26, f32[8,512,512]{2,1,0:T(8,128)} %all-gather.6.cloned.1.call-done, s32[]{:T(128)S(6)} %select_n.107), kind=kOutput, calls=%fused_computation.9 | convolution fusion | flops 6446645248 | bytes 17825802 | tf_op jit(solution)/shard_map/axy,zy->axz/dot_general | solution.py:57
  468.6 52.1 %all-gather.8.cloned.1.call-done = f32[8,512,512]{2,1,0:T(8,128)} async-done(((f32[1,512,512]{2,1,0:T(8,128)}), f32[8,512,512]{2,1,0:T(8,128)}) %all-gather.8.cloned.1.call-update) | async-done | bytes 8388624 | tf_op jit(solution)/shard_map/all_gather | solution.py:10
  523.0 11.7 %cholesky.358 = f32[128,128]{1,0:T(8,128)S(1)} custom-call(f32[128,128]{1,0:T(8,128)S(1)} %cholesky.439), custom_call_target="Cholesky" | custom-call | tf_op jit(solution)/shard_map/jit(cholesky)/cholesky | solution.py:52
  535.5 9.8 %custom-call.31 = f32[1,128,128]{1,2,0:T(8,128)S(1)} custom-call(f32[1,128,128]{2,1,0:T(8,128)S(1)} %get-tuple-element.56), custom_call_target="InvertDiagBlocksLowerTriangular" | custom-call | tf_op jit(solution)/shard_map/jit(cholesky)/cholesky | solution.py:52
  546.1 11.7 %cholesky.377 = f32[128,128]{1,0:T(8,128)S(1)} custom-call(f32[128,128]{1,0:T(8,128)S(1)} %cholesky.443), custom_call_target="Cholesky" | custom-call | tf_op jit(solution)/shard_map/jit(cholesky)/cholesky | solution.py:52
  558.5 10.0 %custom-call.32 = f32[1,128,128]{1,2,0:T(8,128)S(1)} custom-call(f32[1,128,128]{2,1,0:T(8,128)S(1)} %get-tuple-element.53), custom_call_target="InvertDiagBlocksLowerTriangular" | custom-call | tf_op jit(solution)/shard_map/jit(cholesky)/cholesky | solution.py:52
  569.1 11.7 %cholesky.398 = f32[128,128]{1,0:T(8,128)S(1)} custom-call(f32[128,128]{1,0:T(8,128)S(1)} %cholesky.448), custom_call_target="Cholesky" | custom-call | tf_op jit(solution)/shard_map/jit(cholesky)/cholesky | solution.py:52
  581.5 9.8 %custom-call.33 = f32[1,128,128]{1,2,0:T(8,128)S(1)} custom-call(f32[1,128,128]{2,1,0:T(8,128)S(1)} %get-tuple-element.50), custom_call_target="InvertDiagBlocksLowerTriangular" | custom-call | tf_op jit(solution)/shard_map/jit(cholesky)/cholesky | solution.py:52
  591.9 11.9 %cholesky.415 = f32[128,128]{1,0:T(8,128)S(1)} custom-call(f32[128,128]{1,0:T(8,128)S(1)} %convolution_subtract_fusion.8), custom_call_target="Cholesky" | custom-call | tf_op jit(solution)/shard_map/jit(cholesky)/cholesky | solution.py:52
  607.4 8.1 while.5
  615.5 39.3 %custom-call.34 = f32[4,128,128]{1,2,0:T(8,128)S(1)} custom-call(f32[4,128,128]{2,1,0:T(8,128)S(1)} %get-tuple-element.22), custom_call_target="InvertDiagBlocksLowerTriangular" | custom-call | tf_op jit(solution)/shard_map/triangular_solve/custom-call.3 | solution.py:20
  666.1 5.6 fusion.14
  675.3 5.3 copy.36
  680.6 4.9 select_select_fusion
  685.6 161.1 %all-reduce.6.cloned.1.call-done = f32[4,512,512]{2,1,0:T(8,128)} async-done(((f32[4,512,512]{2,1,0:T(8,128)}), f32[4,512,512]{2,1,0:T(8,128)}) %all-reduce.6.cloned.1.call-update) | async-done | bytes 4194320 | tf_op jit(solution)/shard_map/psum | solution.py:15
  849.1 53.1 %all-gather.10.cloned.1.call-done = f32[8,512,512]{2,1,0:T(8,128)} async-done(((f32[1,512,512]{2,1,0:T(8,128)}), f32[8,512,512]{2,1,0:T(8,128)}) %all-gather.10.cloned.1.call-update) | async-done | bytes 8388624 | tf_op jit(solution)/shard_map/all_gather | solution.py:10
  902.1 11.6 %select_bitcast_fusion = f32[4,1,512,512]{3,2,1,0:T(8,128)} fusion(f32[4,512,512]{2,1,0:T(8,128)} %all-reduce.6.cloned.1.call-done, f32[4,512,512]{2,1,0:T(8,128)} %copy-done, pred[4]{0:T(512)(128)(4,1)S(1)} %broadcast_compare_fusion.3, pred[]{:T(512)S(6)} %eq.36, pred[]{:T(512)S(6)} %gt.24, f32[8,512,512]{2,1,0:T(8,128)} %all-gather.10.cloned.1.call-done, ...), kind=kOutput, calls=%fused_computation.10 | convolution fusion | flops 6446645248 | bytes 17825802 | tf_op jit(solution)/shard_map/axy,zy->axz/dot_general | solution.py:57
  (114 shorter events, 70.4 us)
Async XLA Ops:
  6.5 57.0 %all-gather.12.cloned.1.call-start = ((), (), s32[]{:S(2)}) async-start(), calls=%async_computation.5 | async-start | bytes 9437184 | tf_op jit(solution)/shard_map/all_gather | solution.py:10
  8.8 390.2 %all-reduce.4.cloned.1.call-start = ((), (), s32[]{:S(2)}) async-start(), calls=%async_computation | async-start | bytes 8388608 | tf_op jit(solution)/shard_map/psum | solution.py:15
  207.1 6.6 copy-start.2
  237.8 216.6 %all-gather.6.cloned.1.call-start = ((), (), s32[]{:S(2)}) async-start(), calls=%async_computation.1 | async-start | bytes 9437184 | tf_op jit(solution)/shard_map/all_gather | solution.py:10
  401.3 119.3 %all-gather.8.cloned.1.call-start = ((), (), s32[]{:S(2)}) async-start(), calls=%async_computation.2 | async-start | bytes 9437184 | tf_op jit(solution)/shard_map/all_gather | solution.py:10
  464.9 2.0 copy-start
  468.1 378.6 %all-reduce.6.cloned.1.call-start = ((), (), s32[]{:S(2)}) async-start(), calls=%async_computation.3 | async-start | bytes 8388608 | tf_op jit(solution)/shard_map/psum | solution.py:15
  654.9 6.6 copy-start.1
  685.5 216.6 %all-gather.10.cloned.1.call-start = ((), (), s32[]{:S(2)}) async-start(), calls=%async_computation.4 | async-start | bytes 9437184 | tf_op jit(solution)/shard_map/all_gather | solution.py:10
Sparse Core Ops, SparseCore 0:
  9.2 54.2 all-gather.11
  237.9 161.0 all-reduce.3
  401.4 52.9 all-gather.5
  468.2 52.4 all-gather.7
  685.7 161.0 all-reduce.5
  849.2 52.9 all-gather.9
where the time goes:
time: 932 us; the launch traced here: 921 us
  waiting for transfers between devices  535 us (57%)
  other arithmetic  263 us (28%)
  matrix products  61.5 us (7%)
  local copies, waits for them, and re-layouts  40.9 us (4%)
  between operations  19.5 us (2%)
    psum x2, waiting for transfers between devices, spread(): return lax.psum(jnp.where(mine, x, jnp.zeros_like(x)), axis)  322 us
    all_gather x4, waiting for transfers between devices, broadcast(): lax.all_gather(x, axis)  213 us
    another operation x29, other arithmetic, body(): lower_factor = jnp.linalg.cholesky(diag_raw)  169 us
    another operation x7, other arithmetic, factor_blocks(): lax.linalg.triangular_solve(lower_factor, blocks.reshape(count_rows * blo...  84.1 us
    another operation x14, matrix products, factor_blocks(): lax.linalg.triangular_solve(lower_factor, blocks.reshape(count_rows * blo...  35.7 us
    another operation x29, local copies, waits for them, and re-layouts, factor_blocks(): lax.linalg.triangular_solve(lower_factor, blocks.reshape(count_rows * blo...  26.7 us
    dot_general x2, matrix products, body(): jnp.einsum('axy,zy->axz', panel_blocks, cross_block, precision=lax.Precis...  22.1 us
  transfers between devices with their start and end apart: 6, of which 6 were waited for; matrix products, arithmetic and copies ran while one was open for 0% of the time, Pallas kernels for 0%

commit v1 on v0

v1 whole, which is shorter than its diff:
```python
import functools
import jax
import jax.numpy as jnp
from jax import lax
from jax.experimental import pallas as pl
from jax.experimental.pallas import tpu as pltpu
from jax.sharding import PartitionSpec as P

HI = lax.Precision.HIGHEST
F32 = jnp.float32
BF16 = jnp.bfloat16
MESH = pl.DeviceIdType.MESH
B = 512
ROW_SPLIT = 24
NS = 16
Z_ORDER = (0, 1, 7, 2, 6, 3, 5, 4)

R_TS = 0
R_CR = 4
R_CS = 12
R_A0 = 20
R_A1 = 36
R_A2 = 44
R_P1Z = 52
R_P1X = 60
R_P2X = 64
R_P2Z = 96
N_RECV = 128
S_TS = 0
S_CR = 16
S_CS = 24
S_A = 32
S_P1Z = 256
S_P1X = 264
S_P2X = 268
S_P2Z = 300
N_SEND = 332


class Comm:
    def __init__(self, m_ref, tbuf, cbuf, abuf, ssem, rsem, lsem):
        self.m, self.t, self.c, self.a = m_ref, tbuf, cbuf, abuf
        self.ssem, self.rsem, self.lsem = ssem, rsem, lsem
        self.r = lax.axis_index("row")
        self.z = lax.axis_index("col")
        self.x = lax.axis_index("depth")
        self.y = self.r // 2
        self.k = self.r % 2
        self.q = self.z * 4 + self.x
        self.other = self.coord(row=self.r + 1 - 2 * self.k)

    def coord(self, row=None, z=None, x=None):
        return {
            "row": self.r if row is None else row,
            "col": self.z if z is None else z,
            "depth": self.x if x is None else x,
        }

    def remote(self, src, dst, ssem, rsem, to):
        return pltpu.make_async_remote_copy(
            src_ref=src,
            dst_ref=dst,
            send_sem=self.ssem.at[ssem],
            recv_sem=self.rsem.at[rsem],
            device_id=to,
            device_id_type=MESH,
        )

    def wait_recv(self, ref, rsem):
        self.remote(ref, ref, 0, rsem, self.other).wait_recv()

    def wait_send(self, ref, ssem):
        self.remote(ref, ref, ssem, 0, self.other).wait_send()

    def barrier(self):
        sem = pltpu.get_barrier_semaphore()
        r, z, x, y, k, q = self.r, self.z, self.x, self.y, self.k, self.q
        ring = [
            self.coord(row=r + 1 - 2 * k),
            self.coord(row=(r + 2) % 8),
            self.coord(row=(r + 6) % 8),
            self.coord(z=(z + 1) % 8),
            self.coord(z=(z + 7) % 8),
            self.coord(x=(x + 1) % 4),
            self.coord(x=(x + 3) % 4),
        ]
        for to in ring:
            pl.semaphore_signal(sem, inc=1, device_id=to, device_id_type=MESH)
        mine = r == q // 16
        for a in range(4):
            col = 8 * a + r

            @pl.when(jnp.logical_not(mine & (col == q)))
            def _():
                to = self.coord(row=q // 16, z=col // 4, x=col % 4)
                pl.semaphore_signal(sem, inc=1, device_id=to, device_id_type=MESH)

        source = r < 2
        dest = q % 8

        @pl.when(source)
        def _():
            def one(i, carry):
                p = r * 16 + i

                @pl.when(jnp.logical_not((dest == r) & (p == q)))
                def _():
                    to = self.coord(row=dest, z=p // 4, x=p % 4)
                    pl.semaphore_signal(sem, inc=1, device_id=to, device_id_type=MESH)

                return carry

            lax.fori_loop(0, 16, one, 0)

        self.own = mine & (q % 8 == r)
        own = self.own.astype(jnp.int32)
        pl.semaphore_wait(sem, 11 - own + source.astype(jnp.int32) * (16 - own))

    def chunk_c(self, k, i):
        return self.c.at[pl.ds(pl.multiple_of(k * B + i * 64, 64), 64), :]

    def load(self):
        @pl.when(self.r < 2)
        def _():
            dst = self.c.at[pl.ds(pl.multiple_of(self.k * B, B), B), :]
            cp = pltpu.make_async_copy(self.m.at[0, 0], dst, self.lsem.at[0])
            cp.start()
            for b, (xs, ks) in enumerate(((0, 0), (1, 0), (1, 1))):

                @pl.when((self.z == 0) & (self.x == xs) & (self.k == ks))
                def _():
                    ca = pltpu.make_async_copy(self.m.at[0, 0], self.a.at[b], self.lsem.at[1])
                    ca.start()
                    ca.wait()

            cp.wait()

    def ts_piece(self, p, a):
        return self.t.at[pl.ds(pl.multiple_of(p * 32, 32), 32), pl.ds(pl.multiple_of(a * B, B), B)]

    def ts_send(self):
        @pl.when(self.r < 2)
        def _():
            dest = self.q % 8
            a = self.q // 8

            def one(i, carry):
                p = self.r * 16 + i
                src = self.c.at[pl.ds(pl.multiple_of(p * 32, 32), 32), :]
                dst = self.ts_piece(p, a)
                is_own = (dest == self.r) & (p == self.q)

                @pl.when(jnp.logical_not(is_own))
                def _():
                    to = self.coord(row=dest, z=p // 4, x=p % 4)
                    self.remote(src, dst, S_TS + i, R_TS + a, to).start()

                @pl.when(is_own)
                def _():
                    pltpu.make_async_copy(src, dst, self.lsem.at[2]).start()

                return carry

            lax.fori_loop(0, 16, one, 0)

    def ts_wait(self):
        for a in range(4):
            own = self.own & (self.q // 8 == a)

            @pl.when(jnp.logical_not(own))
            def _():
                self.wait_recv(self.ts_piece(self.q, a), R_TS + a)

            @pl.when(own)
            def _():
                ref = self.ts_piece(self.q, a)
                pltpu.make_async_copy(ref, ref, self.lsem.at[2]).wait()

    def ts_finish(self):
        @pl.when(self.r < 2)
        def _():
            dest = self.q % 8

            def one(i, carry):
                p = self.r * 16 + i

                @pl.when(jnp.logical_not((dest == self.r) & (p == self.q)))
                def _():
                    self.wait_send(self.ts_piece(0, 0), S_TS + i)

                return carry

            lax.fori_loop(0, 16, one, 0)

    def c_start(self):
        @pl.when(self.y == 0)
        def _():
            self.c_move(0)
            self.c_move(1)

    def c_pass(self, n):
        @pl.when(self.y != 0)
        def _():
            self.c_move(n)

    def c_move(self, n):
        far = self.y // 3
        h = far if n == 0 else 1 - far
        on = jnp.where(h == 0, self.y != 3, self.y != 1)
        row = (self.r + 2 + 4 * h) % 8

        def one(j, carry):
            i = h * 4 + j
            ref = self.chunk_c(self.k, i)

            @pl.when(self.y != 0)
            def _():
                self.wait_recv(ref, R_CR + i)

            @pl.when(on)
            def _():
                self.remote(ref, ref, S_CR + i, R_CR + i, self.coord(row=row)).start()

            self.remote(ref, ref, S_CS + i, R_CS + i, self.other).start()
            return carry

        lax.fori_loop(0, 4, one, 0)

    def c_finish(self):
        def one(i, carry):
            self.wait_recv(self.chunk_c(1 - self.k, i), R_CS + i)
            self.wait_send(self.chunk_c(self.k, i), S_CS + i)
            h = i // 4

            @pl.when(jnp.where(h == 0, self.y != 3, self.y != 1))
            def _():
                self.wait_send(self.chunk_c(self.k, i), S_CR + i)

            return carry

        lax.fori_loop(0, 8, one, 0)

    A_INFO = ((0, 0, R_A0, 16, 32, 0), (1, 0, R_A1, 8, 64, 16), (1, 1, R_A2, 8, 64, 24))

    def a_children(self, b):
        xs = self.A_INFO[b][0]
        z, y, x, r = self.z, self.y, self.x, self.r
        dx = (x - xs + 4) % 4
        z0 = z == 0
        zy0 = z0 & (y == 0)
        return (
            (z <= 3, self.coord(z=(z + 1) % 8)),
            (z0 | (z >= 6), self.coord(z=(z + 7) % 8)),
            (z0 & (y <= 1), self.coord(row=(r + 2) % 8)),
            (zy0, self.coord(row=(r + 6) % 8)),
            (zy0 & (dx <= 1), self.coord(x=(x + 1) % 4)),
            (zy0 & (dx == 0), self.coord(x=(x + 3) % 4)),
            (None, self.other),
        )

    def a_chunk(self, b, g, j):
        n = self.A_INFO[b][4]
        row = pl.multiple_of(g * 128 + j * n, n)
        lane = 0 if b == 1 else g * 128
        return self.a.at[b, pl.ds(row, n), lane:B]

    def a_loop(self, b, groups, fn):
        per = 128 // self.A_INFO[b][4]
        for g in groups:

            def one(j, carry):
                fn(self.a_chunk(b, g, j), g * per + j)
                return carry

            lax.fori_loop(0, per, one, 0)

    def a_relay(self, b, groups=range(4)):
        xs, ks, rs, s0 = self.A_INFO[b][:3] + self.A_INFO[b][5:]

        @pl.when(self.k == ks)
        def _():
            source = (self.z == 0) & (self.y == 0) & (self.x == xs)

            def one(ref, j):
                @pl.when(jnp.logical_not(source))
                def _():
                    self.wait_recv(ref, rs + j)

                for d, (cond, to) in enumerate(self.a_children(b)):
                    copy = self.remote(ref, ref, S_A + (s0 + j) * 7 + d, rs + j, to)
                    if cond is None:
                        copy.start()
                    else:
                        pl.when(cond)(copy.start)

            self.a_loop(b, groups, one)

    def a_take(self, b, groups=range(4)):
        ks, rs = self.A_INFO[b][1:3]

        @pl.when(self.k != ks)
        def _():
            self.a_loop(b, groups, lambda ref, j: self.wait_recv(ref, rs + j))

    def a_finish(self, blocks=range(3)):
        for b in blocks:
            ks, s0 = self.A_INFO[b][1], self.A_INFO[b][5]

            @pl.when(self.k == ks)
            def _():
                for d, (cond, _) in enumerate(self.a_children(b)):

                    def wait():
                        self.a_loop(b, range(4), lambda ref, j: self.wait_send(ref, S_A + (s0 + j) * 7 + d))

                    if cond is None:
                        wait()
                    else:
                        pl.when(cond)(wait)

    def shard(self, z, x, half):
        p = (z % 8) * 4 + x % 4
        if half == 0:
            return self.t.at[pl.ds(pl.multiple_of(p * 32, 8), ROW_SPLIT), :]
        return self.t.at[pl.ds(pl.multiple_of(p * 32 + ROW_SPLIT, 8), 32 - ROW_SPLIT), :]

    def zto(self, sign):
        return self.coord(z=(self.z + 8 + sign) % 8)

    def xto(self, sign):
        return self.coord(x=(self.x + 4 + sign) % 4)

    def p1z(self, op, sign, s):
        i = s if sign > 0 else 4 + s
        if op == "send":
            ref = self.shard(self.z + 8 - sign * s, self.x, 0)
            self.remote(ref, ref, S_P1Z + i, R_P1Z + i, self.zto(sign)).start()
        elif op == "recv":
            self.wait_recv(self.shard(self.z + 8 - sign * (s + 1), self.x, 0), R_P1Z + i)
        else:
            self.wait_send(self.shard(self.z, self.x, 0), S_P1Z + i)

    def p1x(self, op, sign, s):
        i = s if sign > 0 else 2 + s
        if op == "send":
            ref = self.shard(self.z, self.x + 4 - sign * s, 1)
            self.remote(ref, ref, S_P1X + i, R_P1X + i, self.xto(sign)).start()
        elif op == "recv":
            self.wait_recv(self.shard(self.z, self.x + 4 - sign * (s + 1), 1), R_P1X + i)
        else:
            self.wait_send(self.shard(self.z, self.x, 1), S_P1X + i)

    def p2x(self, op, sign, s, d):
        i = (0 if sign > 0 else 16) + s * 8 + d
        if op == "send":
            ref = self.shard(self.z + d, self.x + 4 - sign * s, 0)
            self.remote(ref, ref, S_P2X + i, R_P2X + i, self.xto(sign)).start()
        elif op == "recv":
            self.wait_recv(self.shard(self.z + d, self.x + 4 - sign * (s + 1), 0), R_P2X + i)
        else:
            self.wait_send(self.shard(self.z, self.x, 0), S_P2X + i)

    def p2z(self, op, sign, s, d):
        i = (0 if sign > 0 else 16) + s * 4 + d
        if op == "send":
            ref = self.shard(self.z + 8 - sign * s, self.x + d, 1)
            self.remote(ref, ref, S_P2Z + i, R_P2Z + i, self.zto(sign)).start()
        elif op == "recv":
            self.wait_recv(self.shard(self.z + 8 - sign * (s + 1), self.x + d, 1), R_P2Z + i)
        else:
            self.wait_send(self.shard(self.z, self.x, 1), S_P2Z + i)

    def p2z_pairs(self, s):
        if s < 3:
            return [(sign, d) for d in range(4) for sign in (1, -1)]
        return [(1, 0), (1, 1), (-1, 2), (-1, 3)]

    def t_stage(self, n):
        if n == 0:
            self.ts_wait()
            for sign in (1, -1):
                self.p1z("send", sign, 0)
                self.p1x("send", sign, 0)
        elif n == 1:
            for sign in (1, -1):
                self.p1z("recv", sign, 0)
                self.p1z("send", sign, 1)
                self.p1x("recv", sign, 0)
            self.p1x("send", 1, 1)
            for d in (0, 1, 7):
                for sign in (1, -1):
                    self.p2x("send", sign, 0, d)
        elif n == 2:
            for sign in (1, -1):
                self.p1z("recv", sign, 1)
                self.p1z("send", sign, 2)
            self.p1x("recv", 1, 1)
            for sign, d in self.p2z_pairs(0):
                self.p2z("send", sign, 0, d)
            for d in (2, 6):
                for sign in (1, -1):
                    self.p2x("send", sign, 0, d)
        elif n == 3:
            for sign in (1, -1):
                self.p1z("recv", sign, 2)
            self.p1z("send", 1, 3)
            for d in (3, 5):
                for sign in (1, -1):
                    self.p2x("send", sign, 0, d)
        elif n == 4:
            self.p1z("recv", 1, 3)
            for sign in (1, -1):
                self.p2x("send", sign, 0, 4)
            for sign, d in self.p2z_pairs(0):
                self.p2z("recv", sign, 0, d)
                self.p2z("send", sign, 1, d)
        elif n == 5:
            self.p2x_pass((0, 1, 7))
        elif n == 6:
            for sign, d in self.p2z_pairs(1):
                self.p2z("recv", sign, 1, d)
                self.p2z("send", sign, 2, d)
        elif n == 7:
            self.p2x_pass((2, 6))
        elif n == 8:
            last = self.p2z_pairs(3)
            for sign, d in self.p2z_pairs(2):
                self.p2z("recv", sign, 2, d)
                if (sign, d) in last:
                    self.p2z("send", sign, 3, d)
        elif n == 9:
            self.p2x_pass((3, 5, 4))
        elif n == 10:
            for d in Z_ORDER:
                self.p2x("recv", 1 if d % 2 == 0 else -1, 1, d)
            for sign, d in self.p2z_pairs(3):
                self.p2z("recv", sign, 3, d)

    def p2x_pass(self, ds):
        for d in ds:
            for sign in (1, -1):
                self.p2x("recv", sign, 0, d)
            self.p2x("send", 1 if d % 2 == 0 else -1, 1, d)

    def t_finish(self):
        self.ts_finish()
        for s in range(4):
            self.p1z("sent", 1, s)
        for s in range(3):
            self.p1z("sent", -1, s)
        self.p1x("sent", 1, 0)
        self.p1x("sent", 1, 1)
        self.p1x("sent", -1, 0)
        for d in range(8):
            self.p2x("sent", 1, 0, d)
            self.p2x("sent", -1, 0, d)
            self.p2x("sent", 1 if d % 2 == 0 else -1, 1, d)
        for s in range(4):
            for sign, d in self.p2z_pairs(s):
                self.p2z("sent", sign, s, d)


def dot(a, b):
    return jnp.dot(a, b, precision=HI, preferred_element_type=F32)


def dot_t(a, b):
    return lax.dot_general(a, b, (((0,), (0,)), ((), ())), precision=HI, preferred_element_type=F32)


def factor128(buf, ns, hook):
    width = buf.shape[1]
    rows = lax.broadcasted_iota(jnp.int32, (ns, 128), 0)
    for s in range(128 // ns):
        base = s * ns
        strip = [buf[base : base + ns, g * 128 : (g + 1) * 128] for g in range(width // 128)]
        cols = [jnp.broadcast_to(strip[0][:, base + j : base + j + 1], (ns, 128)) for j in range(ns)]
        for p in range(ns):
            r = lax.rsqrt(cols[p][p : p + 1, :])
            low = jnp.where(rows > p, cols[p], 0.0) * r
            for g in range(width // 128):
                u = strip[g][p : p + 1, :] * r
                buf[base + p : base + p + 1, g * 128 : (g + 1) * 128] = u
                strip[g] = strip[g] - low * u
            for j in range(p + 1, ns):
                cols[j] = cols[j] - low * (cols[j][p : p + 1, :] * r)
        nxt = base + ns
        if nxt < 128:
            u = buf[base:nxt, :]
            buf[nxt:128, :] = buf[nxt:128, :] - dot_t(u[:, nxt:128], u)
        hook(nxt)


def chol512(wk, buf, ns, hook):
    eye = (lax.broadcasted_iota(jnp.int32, (128, 128), 0) == lax.broadcasted_iota(jnp.int32, (128, 128), 1)).astype(F32)
    r5 = lax.broadcasted_iota(jnp.int32, (512, 512), 0)
    c5 = lax.broadcasted_iota(jnp.int32, (512, 512), 1)
    wk[:, 512:1024] = (r5 == c5).astype(F32)

    def step(kb, carry):
        off = pl.multiple_of(kb * 128, 128)
        buf[:, 0:128] = wk[pl.ds(off, 128), pl.ds(off, 128)]
        buf[:, 128:256] = eye
        factor128(buf, ns, functools.partial(hook, kb))
        new = dot(buf[:, 128:256], wk[pl.ds(off, 128), :])
        wk[pl.ds(off, 128), :] = new
        wk[pl.ds(off, 128), pl.ds(off, 128)] = buf[:, 0:128]

        def upd(j, c):
            o = pl.multiple_of(j * 128, 128)
            left = wk[pl.ds(off, 128), pl.ds(o, 128)]
            wk[pl.ds(o, 128), :] = wk[pl.ds(o, 128), :] - dot_t(left, wk[pl.ds(off, 128), :])
            return c

        lax.fori_loop(kb + 1, 4, upd, 0)
        return carry

    lax.fori_loop(0, 4, step, 0)


def fused_kernel(m_ref, t_ref, c_ref, w_ref, u_ref, a_ref, wk, buf, ssem, rsem, lsem):
    cm = Comm(m_ref, t_ref, c_ref, a_ref, ssem, rsem, lsem)
    cm.load()
    cm.barrier()
    cm.ts_send()
    cm.c_start()
    cm.a_relay(0)
    cm.a_take(0)

    def lead(g):
        cm.a_relay(1, (g,))
        cm.a_relay(2, (g,))

    def rest():
        cm.a_take(1)
        cm.a_take(2)

    plan = [
        (lambda: cm.t_stage(0),),
        (lambda: lead(0),),
        (lambda: cm.t_stage(1),),
        (lambda: lead(1),),
        (lambda: cm.t_stage(2), lambda: cm.c_pass(0)),
        (lambda: lead(2),),
        (lambda: cm.t_stage(3),),
        (lambda: lead(3), rest),
        (lambda: cm.t_stage(4), lambda: cm.c_pass(1)),
        (lambda: cm.t_stage(5),),
        (lambda: cm.t_stage(6),),
        (lambda: cm.t_stage(7),),
        (lambda: cm.t_stage(8),),
        (lambda: cm.t_stage(9),),
        (),
        (),
    ]
    upper = lax.broadcasted_iota(jnp.int32, (512, 512), 0) <= lax.broadcasted_iota(jnp.int32, (512, 512), 1)

    def half(h, c):
        @pl.when(h == 0)
        def _():
            wk[:, 0:512] = a_ref[0]

        @pl.when(h == 1)
        def _():
            u01 = dot(w_ref[0], a_ref[1])
            u_ref[2] = u01
            wk[:, 0:512] = a_ref[2] - dot_t(u01, u01)

        def hook(kb, done):
            if done % 64:
                return
            for i in range(8):
                acts = plan[2 * i + done // 64 - 1]
                if acts:

                    @pl.when(h * 4 + kb == i)
                    def _():
                        for act in acts:
                            act()

        chol512(wk, buf, NS, hook)
        u_ref[h] = jnp.where(upper, wk[:, 0:512], 0.0)
        w_ref[h] = wk[:, 512:1024]
        return c

    lax.fori_loop(0, 2, half, 0)
    cm.t_stage(10)
    cm.c_finish()
    cm.a_finish()
    cm.t_finish()


def fused(m):
    vm = pl.BlockSpec(memory_space=pltpu.VMEM)
    return pl.pallas_call(
        fused_kernel,
        out_shape=(
            jax.ShapeDtypeStruct((1024, 2048), F32),
            jax.ShapeDtypeStruct((1024, 512), F32),
            jax.ShapeDtypeStruct((2, 512, 512), F32),
            jax.ShapeDtypeStruct((3, 512, 512), F32),
        ),
        in_specs=[pl.BlockSpec(memory_space=pl.ANY)],
        out_specs=(vm,) * 4,
        scratch_shapes=[
            pltpu.VMEM((3, 512, 512), F32),
            pltpu.VMEM((512, 1024), F32),
            pltpu.VMEM((128, 256), F32),
            pltpu.SemaphoreType.DMA((N_SEND,)),
            pltpu.SemaphoreType.DMA((N_RECV,)),
            pltpu.SemaphoreType.DMA((3,)),
        ],
        compiler_params=pltpu.CompilerParams(
            collective_id=0, has_side_effects=True, vmem_limit_bytes=50 * 2**20
        ),
    )(m)


def split(v):
    hi = v.astype(BF16)
    return hi, (v - hi.astype(F32)).astype(BF16)


def dot3(a, b, dims):
    (ah, al), (bh, bl) = a, b
    d = functools.partial(lax.dot_general, dimension_numbers=(dims, ((), ())), preferred_element_type=F32)
    return d(al, bh) + d(ah, bl) + d(ah, bh)


NN = ((1,), (0,))
TN = ((0,), (0,))


def solve_pair(w0, w1, u01, top, bottom):
    x0 = dot3(w0, split(top), NN)
    x0s = split(x0)
    x1 = dot3(w1, split(bottom - dot3(u01, x0s, TN)), NN)
    return x0, x1, x0s, split(x1)


def update_kernel(f_ref, t_ref, c_ref, w_ref, u_ref, o_ref, wh, wl, yh, yl):
    a = pl.program_id(0)
    row = lax.axis_index("row")
    col = lax.axis_index("col") * 4 + lax.axis_index("depth")
    block = a * 8 + row

    @pl.when(a == 0)
    def _():
        for n, ref in enumerate((w_ref.at[0], w_ref.at[1], u_ref.at[2])):
            h, l = split(ref[...])
            wh[n] = h
            wl[n] = l

    w0, w1, u01 = ((wh[n], wl[n]) for n in range(3))

    @pl.when((a == 0) & (col >= 2))
    def _():
        _, _, y0, y1 = solve_pair(w0, w1, u01, c_ref[0:512, :], c_ref[512:1024, :])
        yh[0:512, :], yl[0:512, :] = y0
        yh[512:1024, :], yl[512:1024, :] = y1

    x0, x1, x0s, x1s = solve_pair(w0, w1, u01, t_ref[0:512, :], t_ref[512:1024, :])

    @pl.when(col == 0)
    def _():
        @pl.when(block == 0)
        def _():
            o_ref[0] = u_ref[0].T

        @pl.when(block != 0)
        def _():
            o_ref[0] = x0.T

    @pl.when(col == 1)
    def _():
        @pl.when(block == 0)
        def _():
            o_ref[0] = jnp.zeros((B, B), F32)

        @pl.when(block == 1)
        def _():
            o_ref[0] = u_ref[1].T

        @pl.when(block > 1)
        def _():
            o_ref[0] = x1.T

    @pl.when(col >= 2)
    def _():
        @pl.when(block <= 1)
        def _():
            o_ref[0] = jnp.zeros((B, B), F32)

        @pl.when(block > 1)
        def _():
            s = dot3(x0s, (yh[0:512, :], yl[0:512, :]), TN) + dot3(x1s, (yh[512:1024, :], yl[512:1024, :]), TN)
            o_ref[0] = f_ref[0] - s


def update(f, t, c, w, u):
    whole = lambda *shape: pl.BlockSpec(shape, lambda a: (0,) * len(shape))
    return pl.pallas_call(
        update_kernel,
        grid=(4,),
        out_shape=jax.ShapeDtypeStruct((4, B, B), F32),
        in_specs=[
            pl.BlockSpec((1, B, B), lambda a: (a, 0, 0)),
            pl.BlockSpec((1024, B), lambda a: (0, a)),
            whole(1024, 512),
            whole(2, B, B),
            whole(3, B, B),
        ],
        out_specs=pl.BlockSpec((1, B, B), lambda a: (a, 0, 0)),
        scratch_shapes=[
            pltpu.VMEM((3, B, B), BF16),
            pltpu.VMEM((3, B, B), BF16),
            pltpu.VMEM((1024, B), BF16),
            pltpu.VMEM((1024, B), BF16),
        ],
        compiler_params=pltpu.CompilerParams(
            dimension_semantics=("arbitrary",), vmem_limit_bytes=50 * 2**20
        ),
    )(f, t, c, w, u)


def body(matrix):
    t, c, w, u = fused(matrix)
    return update(matrix[:, 0], t, c, w, u)[:, None]


def solution(mesh):
    spec = P(None, "row", None, ("col", "depth"))
    return jax.shard_map(body, mesh=mesh, in_specs=(spec,), out_specs=spec, check_vma=False)
```

time: 932 us -> 214 us (0.23)
  the two profiles are of different devices: /device:TPU:19 before, /device:TPU:108 now
where the time goes in v1:
time: 214 us
  Pallas kernels  214 us (100%)
    pallas_call x1, Pallas kernels, fused(): pl.pallas_call(fused_kernel, out_shape=(jax.ShapeDtypeStruct((1024, 2048)...  188 us
    pallas_call x1, Pallas kernels, update(): pl.pallas_call(update_kernel, grid=(4,), out_shape=jax.ShapeDtypeStruct((...  26.4 us

profile of v1, /device:TPU:108, one launch (start us, length us, event | category | flops | bytes accessed | tf_op | source)
XLA Modules:
  0.0 214.0 jit_solution(10744815001893953035)
XLA Ops:
  0.0 187.5 %shard_map.17 = (f32[1024,2048]{1,0:T(8,128)}, f32[1024,512]{1,0:T(8,128)S(1)}, f32[2,512,512]{2,1,0:T(8,128)}, f32[3,512,512]{2,1,0:T(8,128)}) custom-call(f32[4,1,512,512]{3,2,1,0:T(8,128)} %m_ref.1), custom_call_target="tpu_custom_call" | custom-call | tf_op jit(solution)/shard_map/pallas_call | solution.py:595
  187.5 26.4 %shard_map.18 = f32[4,512,512]{2,1,0:T(8,128)} custom-call(f32[4,512,512]{2,1,0:T(8,128)} %bitcast.4, f32[1024,2048]{1,0:T(8,128)} %get-tuple-element.9.t_ref, f32[1024,512]{1,0:T(8,128)S(1)} %get-tuple-element.10.c_ref, f32[2,512,512]{2,1,0:T(8,128)} %get-tuple-element.11.w_ref, f32[3,512,512]{2,1,0:T(8,128)} %get-tuple-element.12.u_ref), custom_call_target="tpu_custom_call" | custom-call | tf_op jit(solution)/shard_map/pallas_call | solution.py:702

commit v2 on v1

--- a/solution.py
+++ b/solution.py
@@ -25,7 +25,8 @@
 R_P1X = 60
 R_P2X = 64
 R_P2Z = 96
-N_RECV = 128
+R_W = 128
+N_RECV = 134
 S_TS = 0
 S_CR = 16
 S_CS = 24
@@ -34,7 +35,8 @@
 S_P1X = 264
 S_P2X = 268
 S_P2Z = 300
-N_SEND = 332
+S_W = 332
+N_SEND = 338
 
 
 class Comm:
@@ -125,7 +127,7 @@
             dst = self.c.at[pl.ds(pl.multiple_of(self.k * B, B), B), :]
             cp = pltpu.make_async_copy(self.m.at[0, 0], dst, self.lsem.at[0])
             cp.start()
-            for b, (xs, ks) in enumerate(((0, 0), (1, 0), (1, 1))):
+            for b, (xs, ks) in enumerate(((0, 0), (0, 1), (1, 1))):
 
                 @pl.when((self.z == 0) & (self.x == xs) & (self.k == ks))
                 def _():
@@ -199,9 +201,16 @@
             self.c_move(1)
 
     def c_pass(self, n):
-        @pl.when(self.y != 0)
+        @pl.when(self.y % 2 == 1)
         def _():
             self.c_move(n)
+
+        if n == 0:
+
+            @pl.when(self.y == 2)
+            def _():
+                self.c_move(0)
+                self.c_move(1)
 
     def c_move(self, n):
         far = self.y // 3
@@ -240,23 +249,24 @@
 
         lax.fori_loop(0, 8, one, 0)
 
-    A_INFO = ((0, 0, R_A0, 16, 32, 0), (1, 0, R_A1, 8, 64, 16), (1, 1, R_A2, 8, 64, 24))
+    A_INFO = ((0, 0, R_A0, 16, 32, 0), (0, 1, R_A1, 8, 64, 16), (1, 1, R_A2, 8, 64, 24))
 
     def a_children(self, b):
         xs = self.A_INFO[b][0]
         z, y, x, r = self.z, self.y, self.x, self.r
         dx = (x - xs + 4) % 4
-        z0 = z == 0
-        zy0 = z0 & (y == 0)
+        z0, y0 = z == 0, y == 0
+        on_x = y0 if b == 1 else y0 & z0
+        on_z = y0 & (dx == 0) if b == 1 else z >= 0
+        on_y = z >= 0 if b == 1 else z0
         return (
-            (z <= 3, self.coord(z=(z + 1) % 8)),
-            (z0 | (z >= 6), self.coord(z=(z + 7) % 8)),
-            (z0 & (y <= 1), self.coord(row=(r + 2) % 8)),
-            (zy0, self.coord(row=(r + 6) % 8)),
-            (zy0 & (dx <= 1), self.coord(x=(x + 1) % 4)),
-            (zy0 & (dx == 0), self.coord(x=(x + 3) % 4)),
-            (None, self.other),
-        )
+            (on_z & (z <= 3), self.coord(z=(z + 1) % 8)),
+            (on_z & (z0 | (z >= 6)), self.coord(z=(z + 7) % 8)),
+            (on_y & (y <= 1), self.coord(row=(r + 2) % 8)),
+            (on_y & y0, self.coord(row=(r + 6) % 8)),
+            (on_x & (dx <= 1), self.coord(x=(x + 1) % 4)),
+            (on_x & (dx == 0), self.coord(x=(x + 3) % 4)),
+        ) + (((None, self.other),) if b else ())
 
     def a_chunk(self, b, g, j):
         n = self.A_INFO[b][4]
@@ -308,15 +318,21 @@
 
             @pl.when(self.k == ks)
             def _():
-                for d, (cond, _) in enumerate(self.a_children(b)):
-
-                    def wait():
-                        self.a_loop(b, range(4), lambda ref, j: self.wait_send(ref, S_A + (s0 + j) * 7 + d))
-
-                    if cond is None:
-                        wait()
-                    else:
-                        pl.when(cond)(wait)
+                def one(ref, j):
+                    for d, (cond, _) in enumerate(self.a_children(b)):
+                        copy = self.remote(ref, ref, S_A + (s0 + j) * 7 + d, 0, self.other)
+                        if cond is None:
+                            copy.wait_send()
+                        else:
+                            pl.when(cond)(copy.wait_send)
+
+                self.a_loop(b, range(4), one)
+
+    def factors(self, w, u, z):
+        return (w.at[0], w.at[1], u.at[0], u.at[1], u.at[2], z)
+
+    def give(self, refs, n):
+        self.remote(refs[n], refs[n], S_W + n, R_W + n, self.other).start()
 
     def shard(self, z, x, half):
         p = (z % 8) * 4 + x % 4
@@ -518,38 +534,79 @@
     lax.fori_loop(0, 4, step, 0)
 
 
-def fused_kernel(m_ref, t_ref, c_ref, w_ref, u_ref, a_ref, wk, buf, ssem, rsem, lsem):
+def column_solve(c_ref, w_ref, u_ref, z_ref):
+    def chunk(n, carry):
+        lanes = pl.ds(pl.multiple_of(n * 256, 256), 256)
+        y0 = dot(w_ref[0], c_ref[0:512, lanes])
+        y1 = dot(w_ref[1], c_ref[512:1024, lanes] - dot_t(u_ref[2], y0))
+        z1 = dot_t(w_ref[1], y1)
+        z0 = dot_t(w_ref[0], y0 - dot(u_ref[2], z1))
+        z_ref[0:512, lanes] = z0
+        z_ref[512:1024, lanes] = z1
+        return carry
+
+    lax.fori_loop(0, 2, chunk, 0)
+
+
+def fused_kernel(m_ref, t_ref, zh_ref, zl_ref, w_ref, u_ref, c_ref, a_ref, z_ref, wk, buf, ssem, rsem, lsem):
     cm = Comm(m_ref, t_ref, c_ref, a_ref, ssem, rsem, lsem)
+    refs = cm.factors(w_ref, u_ref, z_ref)
     cm.load()
     cm.barrier()
     cm.ts_send()
     cm.c_start()
-    cm.a_relay(0)
-    cm.a_take(0)
-
-    def lead(g):
-        cm.a_relay(1, (g,))
-        cm.a_relay(2, (g,))
-
+
+    @pl.when(cm.k == 1)
+    def _():
+        cm.a_relay(1)
+        cm.a_relay(2)
+        for n in range(11):
+            cm.t_stage(n)
+            if n in (2, 5):
+                cm.c_pass(n // 4)
+        cm.c_finish()
+        for n, ref in enumerate(refs):
+            cm.wait_recv(ref, R_W + n)
+
+    @pl.when(cm.k == 0)
+    def _():
+        cm.a_relay(0)
+        factor(cm, refs, a_ref, w_ref, u_ref, wk, buf)
+        cm.c_finish()
+        column_solve(c_ref, w_ref, u_ref, z_ref)
+        cm.t_stage(10)
+        cm.give(refs, 5)
+        for n, ref in enumerate(refs):
+            cm.wait_send(ref, S_W + n)
+
+    zh_ref[...], zl_ref[...] = split(z_ref[...])
+    cm.a_finish()
+    cm.t_finish()
+
+
+def factor(cm, refs, a_ref, w_ref, u_ref, wk, buf):
     def rest():
         cm.a_take(1)
         cm.a_take(2)
 
+    T = lambda n: (functools.partial(cm.t_stage, n),)
+    C = lambda n: (functools.partial(cm.c_pass, n),)
+    R = (rest,)
     plan = [
-        (lambda: cm.t_stage(0),),
-        (lambda: lead(0),),
-        (lambda: cm.t_stage(1),),
-        (lambda: lead(1),),
-        (lambda: cm.t_stage(2), lambda: cm.c_pass(0)),
-        (lambda: lead(2),),
-        (lambda: cm.t_stage(3),),
-        (lambda: lead(3), rest),
-        (lambda: cm.t_stage(4), lambda: cm.c_pass(1)),
-        (lambda: cm.t_stage(5),),
-        (lambda: cm.t_stage(6),),
-        (lambda: cm.t_stage(7),),
-        (lambda: cm.t_stage(8),),
-        (lambda: cm.t_stage(9),),
+        T(0),
+        T(1),
+        T(2),
+        T(3),
+        C(0) + T(4),
+        (),
+        T(5),
+        R,
+        T(6) + C(1),
+        T(7),
+        (),
+        T(8),
+        (),
+        T(9),
         (),
         (),
     ]
@@ -562,7 +619,7 @@
 
         @pl.when(h == 1)
         def _():
-            u01 = dot(w_ref[0], a_ref[1])
+            u01 = lax.dot_general(w_ref[0], a_ref[1], (((1,), (1,)), ((), ())), precision=HI, preferred_element_type=F32)
             u_ref[2] = u01
             wk[:, 0:512] = a_ref[2] - dot_t(u01, u01)
 
@@ -584,10 +641,8 @@
         return c
 
     lax.fori_loop(0, 2, half, 0)
-    cm.t_stage(10)
-    cm.c_finish()
-    cm.a_finish()
-    cm.t_finish()
+    for n in range(5):
+        cm.give(refs, n)
 
 
 def fused(m):
@@ -596,14 +651,17 @@
         fused_kernel,
         out_shape=(
             jax.ShapeDtypeStruct((1024, 2048), F32),
-            jax.ShapeDtypeStruct((1024, 512), F32),
+            jax.ShapeDtypeStruct((1024, 512), BF16),
+            jax.ShapeDtypeStruct((1024, 512), BF16),
             jax.ShapeDtypeStruct((2, 512, 512), F32),
             jax.ShapeDtypeStruct((3, 512, 512), F32),
         ),
         in_specs=[pl.BlockSpec(memory_space=pl.ANY)],
-        out_specs=(vm,) * 4,
+        out_specs=(vm,) * 5,
         scratch_shapes=[
+            pltpu.VMEM((1024, 512), F32),
             pltpu.VMEM((3, 512, 512), F32),
+            pltpu.VMEM((1024, 512), F32),
             pltpu.VMEM((512, 1024), F32),
             pltpu.VMEM((128, 256), F32),
             pltpu.SemaphoreType.DMA((N_SEND,)),
@@ -631,73 +689,38 @@
 TN = ((0,), (0,))
 
 
-def solve_pair(w0, w1, u01, top, bottom):
-    x0 = dot3(w0, split(top), NN)
-    x0s = split(x0)
-    x1 = dot3(w1, split(bottom - dot3(u01, x0s, TN)), NN)
-    return x0, x1, x0s, split(x1)
-
-
-def update_kernel(f_ref, t_ref, c_ref, w_ref, u_ref, o_ref, wh, wl, yh, yl):
+def update_kernel(f_ref, t_ref, zh_ref, zl_ref, w_ref, u_ref, o_ref):
     a = pl.program_id(0)
     row = lax.axis_index("row")
     col = lax.axis_index("col") * 4 + lax.axis_index("depth")
     block = a * 8 + row
 
-    @pl.when(a == 0)
+    def x0():
+        return dot3(split(w_ref[0]), split(t_ref[0:512, :]), NN)
+
+    @pl.when((col >= 2) & (block > 1))
     def _():
-        for n, ref in enumerate((w_ref.at[0], w_ref.at[1], u_ref.at[2])):
-            h, l = split(ref[...])
-            wh[n] = h
-            wl[n] = l
-
-    w0, w1, u01 = ((wh[n], wl[n]) for n in range(3))
-
-    @pl.when((a == 0) & (col >= 2))
+        o_ref[0] = f_ref[0] - dot3(split(t_ref[...]), (zh_ref[...], zl_ref[...]), TN)
+
+    @pl.when(block < jnp.minimum(col, 2))
     def _():
-        _, _, y0, y1 = solve_pair(w0, w1, u01, c_ref[0:512, :], c_ref[512:1024, :])
-        yh[0:512, :], yl[0:512, :] = y0
-        yh[512:1024, :], yl[512:1024, :] = y1
-
-    x0, x1, x0s, x1s = solve_pair(w0, w1, u01, t_ref[0:512, :], t_ref[512:1024, :])
-
-    @pl.when(col == 0)
+        o_ref[0] = jnp.zeros((B, B), F32)
+
+    @pl.when((block == col) & (col < 2))
     def _():
-        @pl.when(block == 0)
-        def _():
-            o_ref[0] = u_ref[0].T
-
-        @pl.when(block != 0)
-        def _():
-            o_ref[0] = x0.T
-
-    @pl.when(col == 1)
+        o_ref[0] = u_ref[jnp.minimum(col, 1)].T
+
+    @pl.when((col == 0) & (block > 0))
     def _():
-        @pl.when(block == 0)
-        def _():
-            o_ref[0] = jnp.zeros((B, B), F32)
-
-        @pl.when(block == 1)
-        def _():
-            o_ref[0] = u_ref[1].T
-
-        @pl.when(block > 1)
-        def _():
-            o_ref[0] = x1.T
-
-    @pl.when(col >= 2)
+        o_ref[0] = x0().T
+
+    @pl.when((col == 1) & (block > 1))
     def _():
-        @pl.when(block <= 1)
-        def _():
-            o_ref[0] = jnp.zeros((B, B), F32)
-
-        @pl.when(block > 1)
-        def _():
-            s = dot3(x0s, (yh[0:512, :], yl[0:512, :]), TN) + dot3(x1s, (yh[512:1024, :], yl[512:1024, :]), TN)
-            o_ref[0] = f_ref[0] - s
-
-
-def update(f, t, c, w, u):
+        rest = t_ref[512:1024, :] - dot3(split(u_ref[2]), split(x0()), TN)
+        o_ref[0] = dot3(split(w_ref[1]), split(rest), NN).T
+
+
+def update(f, t, zh, zl, w, u):
     whole = lambda *shape: pl.BlockSpec(shape, lambda a: (0,) * len(shape))
     return pl.pallas_call(
         update_kernel,
@@ -706,26 +729,20 @@
         in_specs=[
             pl.BlockSpec((1, B, B), lambda a: (a, 0, 0)),
             pl.BlockSpec((1024, B), lambda a: (0, a)),
-            whole(1024, 512),
+            whole(1024, B),
+            whole(1024, B),
             whole(2, B, B),
             whole(3, B, B),
         ],
         out_specs=pl.BlockSpec((1, B, B), lambda a: (a, 0, 0)),
-        scratch_shapes=[
-            pltpu.VMEM((3, B, B), BF16),
-            pltpu.VMEM((3, B, B), BF16),
-            pltpu.VMEM((1024, B), BF16),
-            pltpu.VMEM((1024, B), BF16),
-        ],
         compiler_params=pltpu.CompilerParams(
             dimension_semantics=("arbitrary",), vmem_limit_bytes=50 * 2**20
         ),
-    )(f, t, c, w, u)
+    )(f, t, zh, zl, w, u)
 
 
 def body(matrix):
-    t, c, w, u = fused(matrix)
-    return update(matrix[:, 0], t, c, w, u)[:, None]
+    return update(matrix[:, 0], *fused(matrix))[:, None]
 
 
 def solution(mesh):

time: 214 us -> 179 us (0.84)
  the two profiles are of different devices: /device:TPU:108 before, /device:TPU:19 now
where the time goes in v2:
time: 179 us; the launch traced here: 178 us
  Pallas kernels  178 us (99%)
    pallas_call x1, Pallas kernels, fused(): pl.pallas_call(fused_kernel, out_shape=(jax.ShapeDtypeStruct((1024, 2048)...  162 us
    pallas_call x1, Pallas kernels, update(): pl.pallas_call(update_kernel, grid=(4,), out_shape=jax.ShapeDtypeStruct((...  16.9 us

profile of v2, /device:TPU:19, one launch (start us, length us, event | category | flops | bytes accessed | tf_op | source)
XLA Modules:
  0.0 178.5 jit_solution(14621927428300813608)
XLA Ops:
  0.0 161.5 %shard_map.17 = (f32[1024,2048]{1,0:T(8,128)}, bf16[1024,512]{1,0:T(8,128)(2,1)S(1)}, bf16[1024,512]{1,0:T(8,128)(2,1)S(1)}, f32[2,512,512]{2,1,0:T(8,128)}, f32[3,512,512]{2,1,0:T(8,128)}) custom-call(f32[4,1,512,512]{3,2,1,0:T(8,128)} %m_ref.1), custom_call_target="tpu_custom_call" | custom-call | tf_op jit(solution)/shard_map/pallas_call | solution.py:650
  161.6 16.9 %shard_map.18 = f32[4,512,512]{2,1,0:T(8,128)} custom-call(f32[4,512,512]{2,1,0:T(8,128)} %bitcast.4, f32[1024,2048]{1,0:T(8,128)} %get-tuple-element.10.t_ref, bf16[1024,512]{1,0:T(8,128)(2,1)S(1)} %get-tuple-element.11.zh_ref, bf16[1024,512]{1,0:T(8,128)(2,1)S(1)} %get-tuple-element.12.zl_ref, f32[2,512,512]{2,1,0:T(8,128)} %get-tuple-element.13.w_ref, ...), custom_call_target="tpu_custom_call" | custom-call | tf_op jit(solution)/shard_map/pallas_call | solution.py:725

commit v3 on v2

--- a/solution.py
+++ b/solution.py
@@ -328,8 +328,8 @@
 
                 self.a_loop(b, range(4), one)
 
-    def factors(self, w, u, z):
-        return (w.at[0], w.at[1], u.at[0], u.at[1], u.at[2], z)
+    def factors(self, w, u):
+        return (w.at[0], w.at[1], u.at[2], u.at[1])
 
     def give(self, refs, n):
         self.remote(refs[n], refs[n], S_W + n, R_W + n, self.other).start()
@@ -534,23 +534,23 @@
     lax.fori_loop(0, 4, step, 0)
 
 
-def column_solve(c_ref, w_ref, u_ref, z_ref):
-    def chunk(n, carry):
-        lanes = pl.ds(pl.multiple_of(n * 256, 256), 256)
-        y0 = dot(w_ref[0], c_ref[0:512, lanes])
-        y1 = dot(w_ref[1], c_ref[512:1024, lanes] - dot_t(u_ref[2], y0))
-        z1 = dot_t(w_ref[1], y1)
-        z0 = dot_t(w_ref[0], y0 - dot(u_ref[2], z1))
-        z_ref[0:512, lanes] = z0
-        z_ref[512:1024, lanes] = z1
-        return carry
-
-    lax.fori_loop(0, 2, chunk, 0)
-
-
-def fused_kernel(m_ref, t_ref, zh_ref, zl_ref, w_ref, u_ref, c_ref, a_ref, z_ref, wk, buf, ssem, rsem, lsem):
+def column_solve(cm, c_ref, w_ref, u_ref, z_ref):
+    lanes = pl.ds(pl.multiple_of(cm.k * 256, 256), 256)
+    row = lax.broadcasted_iota(jnp.int32, (B, 256), 0)
+    eye = (row == lax.broadcasted_iota(jnp.int32, (B, 256), 1) + cm.k * 256).astype(F32)
+    col = jnp.zeros((B, 256), jnp.int32) + cm.q
+    y0 = dot(w_ref[0], c_ref[0:512, lanes])
+    y1 = dot(w_ref[1], c_ref[512:1024, lanes] - dot_t(u_ref[2], y0))
+    y0 = jnp.where(col >= 2, y0, jnp.where(col == 0, eye, 0.0))
+    y1 = jnp.where(col >= 2, y1, jnp.where(col == 1, eye, 0.0))
+    z1 = dot_t(w_ref[1], y1)
+    z_ref[512:1024, lanes] = z1
+    z_ref[0:512, lanes] = dot_t(w_ref[0], y0 - dot(u_ref[2], z1))
+
+
+def fused_kernel(m_ref, t_ref, zh_ref, zl_ref, u_ref, w_ref, c_ref, a_ref, z_ref, wk, buf, ssem, rsem, lsem):
     cm = Comm(m_ref, t_ref, c_ref, a_ref, ssem, rsem, lsem)
-    refs = cm.factors(w_ref, u_ref, z_ref)
+    refs = cm.factors(w_ref, u_ref)
     cm.load()
     cm.barrier()
     cm.ts_send()
@@ -560,11 +560,10 @@
     def _():
         cm.a_relay(1)
         cm.a_relay(2)
-        for n in range(11):
+        for n in range(10):
             cm.t_stage(n)
             if n in (2, 5):
                 cm.c_pass(n // 4)
-        cm.c_finish()
         for n, ref in enumerate(refs):
             cm.wait_recv(ref, R_W + n)
 
@@ -572,16 +571,24 @@
     def _():
         cm.a_relay(0)
         factor(cm, refs, a_ref, w_ref, u_ref, wk, buf)
-        cm.c_finish()
-        column_solve(c_ref, w_ref, u_ref, z_ref)
-        cm.t_stage(10)
-        cm.give(refs, 5)
+
+    cm.c_finish()
+    column_solve(cm, c_ref, w_ref, u_ref, z_ref)
+    cm.t_stage(10)
+    mine = z_ref.at[:, pl.ds(pl.multiple_of(cm.k * 256, 256), 256)]
+    theirs = z_ref.at[:, pl.ds(pl.multiple_of(256 - cm.k * 256, 256), 256)]
+    cm.remote(mine, mine, S_W + 4, R_W + 4, cm.other).start()
+    cm.a_finish()
+    cm.t_finish()
+
+    @pl.when(cm.k == 0)
+    def _():
         for n, ref in enumerate(refs):
             cm.wait_send(ref, S_W + n)
 
+    cm.wait_send(mine, S_W + 4)
+    cm.wait_recv(theirs, R_W + 4)
     zh_ref[...], zl_ref[...] = split(z_ref[...])
-    cm.a_finish()
-    cm.t_finish()
 
 
 def factor(cm, refs, a_ref, w_ref, u_ref, wk, buf):
@@ -641,7 +648,7 @@
         return c
 
     lax.fori_loop(0, 2, half, 0)
-    for n in range(5):
+    for n in range(4):
         cm.give(refs, n)
 
 
@@ -653,12 +660,12 @@
             jax.ShapeDtypeStruct((1024, 2048), F32),
             jax.ShapeDtypeStruct((1024, 512), BF16),
             jax.ShapeDtypeStruct((1024, 512), BF16),
-            jax.ShapeDtypeStruct((2, 512, 512), F32),
             jax.ShapeDtypeStruct((3, 512, 512), F32),
         ),
         in_specs=[pl.BlockSpec(memory_space=pl.ANY)],
-        out_specs=(vm,) * 5,
+        out_specs=(vm,) * 4,
         scratch_shapes=[
+            pltpu.VMEM((2, 512, 512), F32),
             pltpu.VMEM((1024, 512), F32),
             pltpu.VMEM((3, 512, 512), F32),
             pltpu.VMEM((1024, 512), F32),
@@ -689,18 +696,17 @@
 TN = ((0,), (0,))
 
 
-def update_kernel(f_ref, t_ref, zh_ref, zl_ref, w_ref, u_ref, o_ref):
+def update_kernel(f_ref, t_ref, zh_ref, zl_ref, u_ref, o_ref):
     a = pl.program_id(0)
     row = lax.axis_index("row")
     col = lax.axis_index("col") * 4 + lax.axis_index("depth")
     block = a * 8 + row
 
-    def x0():
-        return dot3(split(w_ref[0]), split(t_ref[0:512, :]), NN)
-
-    @pl.when((col >= 2) & (block > 1))
+    @pl.when(block > jnp.minimum(col, 1))
     def _():
-        o_ref[0] = f_ref[0] - dot3(split(t_ref[...]), (zh_ref[...], zl_ref[...]), TN)
+        s = dot3(split(t_ref[...]), (zh_ref[...], zl_ref[...]), TN)
+        trailing = jnp.zeros((B, B), jnp.int32) + col >= 2
+        o_ref[0] = jnp.where(trailing, f_ref[0] - s, s)
 
     @pl.when(block < jnp.minimum(col, 2))
     def _():
@@ -710,17 +716,8 @@
     def _():
         o_ref[0] = u_ref[jnp.minimum(col, 1)].T
 
-    @pl.when((col == 0) & (block > 0))
-    def _():
-        o_ref[0] = x0().T
-
-    @pl.when((col == 1) & (block > 1))
-    def _():
-        rest = t_ref[512:1024, :] - dot3(split(u_ref[2]), split(x0()), TN)
-        o_ref[0] = dot3(split(w_ref[1]), split(rest), NN).T
-
-
-def update(f, t, zh, zl, w, u):
+
+def update(f, t, zh, zl, u):
     whole = lambda *shape: pl.BlockSpec(shape, lambda a: (0,) * len(shape))
     return pl.pallas_call(
         update_kernel,
@@ -732,13 +729,12 @@
             whole(1024, B),
             whole(1024, B),
             whole(2, B, B),
-            whole(3, B, B),
         ],
         out_specs=pl.BlockSpec((1, B, B), lambda a: (a, 0, 0)),
         compiler_params=pltpu.CompilerParams(
             dimension_semantics=("arbitrary",), vmem_limit_bytes=50 * 2**20
         ),
-    )(f, t, zh, zl, w, u)
+    )(f, t, zh, zl, u)
 
 
 def body(matrix):

time: 179 us -> 170 us (0.950); the launches traced: 178 us -> 167 us
  Pallas kernels: 178 us -> 167 us
    pallas_call x1, Pallas kernels: 162 us -> 155 us  [fused(): pl.pallas_call(fused_kernel, out_shape=(jax.ShapeDtypeStruct((1024, 2048)...]
    pallas_call x1, Pallas kernels: 16.9 us -> 11.8 us  [update(): pl.pallas_call(update_kernel, grid=(4,), out_shape=jax.ShapeDtypeStruct((...]
where the time goes in v3:
time: 170 us; the launch traced here: 167 us
  Pallas kernels  167 us (98%)
    pallas_call x1, Pallas kernels, fused(): pl.pallas_call(fused_kernel, out_shape=(jax.ShapeDtypeStruct((1024, 2048)...  155 us
    pallas_call x1, Pallas kernels, update(): pl.pallas_call(update_kernel, grid=(4,), out_shape=jax.ShapeDtypeStruct((...  11.8 us

profile of v3, /device:TPU:19, one launch (start us, length us, event | category | flops | bytes accessed | tf_op | source)
XLA Modules:
  0.0 167.0 jit_solution(10350201053965774297)
XLA Ops:
  0.0 155.2 %shard_map.17 = (f32[1024,2048]{1,0:T(8,128)}, bf16[1024,512]{1,0:T(8,128)(2,1)S(1)}, bf16[1024,512]{1,0:T(8,128)(2,1)S(1)}, f32[3,512,512]{2,1,0:T(8,128)}) custom-call(f32[4,1,512,512]{3,2,1,0:T(8,128)} %m_ref.1), custom_call_target="tpu_custom_call" | custom-call | tf_op jit(solution)/shard_map/pallas_call | solution.py:657
  155.2 11.8 %shard_map.18 = f32[4,512,512]{2,1,0:T(8,128)} custom-call(f32[4,512,512]{2,1,0:T(8,128)} %bitcast.4, f32[1024,2048]{1,0:T(8,128)} %get-tuple-element.9.t_ref, bf16[1024,512]{1,0:T(8,128)(2,1)S(1)} %get-tuple-element.10.zh_ref, bf16[1024,512]{1,0:T(8,128)(2,1)S(1)} %get-tuple-element.11.zl_ref, f32[3,512,512]{2,1,0:T(8,128)} %get-tuple-element.12.u_ref), custom_call_target="tpu_custom_call" | custom-call | tf_op jit(solution)/shard_map/pallas_call | solution.py:722

commit v4 on v3

--- a/solution.py
+++ b/solution.py
@@ -601,21 +601,21 @@
     R = (rest,)
     plan = [
         T(0),
+        (),
         T(1),
+        (),
         T(2),
-        T(3),
-        C(0) + T(4),
         (),
-        T(5),
+        T(3) + C(0),
         R,
-        T(6) + C(1),
+        T(4),
+        T(5) + C(1),
+        (),
+        T(6),
+        (),
         T(7),
-        (),
         T(8),
-        (),
         T(9),
-        (),
-        (),
     ]
     upper = lax.broadcasted_iota(jnp.int32, (512, 512), 0) <= lax.broadcasted_iota(jnp.int32, (512, 512), 1)
 

time: 170 us -> 158 us (0.929)
  the two profiles are of different devices: /device:TPU:19 before, /device:TPU:113 now
where the time goes in v4:
time: 158 us
  Pallas kernels  158 us (100%)
    pallas_call x1, Pallas kernels, fused(): pl.pallas_call(fused_kernel, out_shape=(jax.ShapeDtypeStruct((1024, 2048)...  146 us
    pallas_call x1, Pallas kernels, update(): pl.pallas_call(update_kernel, grid=(4,), out_shape=jax.ShapeDtypeStruct((...  11.8 us

profile of v4, /device:TPU:113, one launch (start us, length us, event | category | flops | bytes accessed | tf_op | source)
XLA Modules:
  0.0 157.9 jit_solution(4859336936825734979)
XLA Ops:
  0.0 146.1 %shard_map.17 = (f32[1024,2048]{1,0:T(8,128)}, bf16[1024,512]{1,0:T(8,128)(2,1)S(1)}, bf16[1024,512]{1,0:T(8,128)(2,1)S(1)}, f32[3,512,512]{2,1,0:T(8,128)}) custom-call(f32[4,1,512,512]{3,2,1,0:T(8,128)} %m_ref.1), custom_call_target="tpu_custom_call" | custom-call | tf_op jit(solution)/shard_map/pallas_call | solution.py:657
  146.1 11.8 %shard_map.18 = f32[4,512,512]{2,1,0:T(8,128)} custom-call(f32[4,512,512]{2,1,0:T(8,128)} %bitcast.4, f32[1024,2048]{1,0:T(8,128)} %get-tuple-element.9.t_ref, bf16[1024,512]{1,0:T(8,128)(2,1)S(1)} %get-tuple-element.10.zh_ref, bf16[1024,512]{1,0:T(8,128)(2,1)S(1)} %get-tuple-element.11.zl_ref, f32[3,512,512]{2,1,0:T(8,128)} %get-tuple-element.12.u_ref), custom_call_target="tpu_custom_call" | custom-call | tf_op jit(solution)/shard_map/pallas_call | solution.py:722
